TPU v7x, 32 devices: a whole 2x2x4 slice. The times are simulated.
32 devices in a mesh: depth: 16 (over z, y, x), spec: 2 (over core).
Axes of the slice: x: 2, y: 2, z: 4, core: 2. Of those that a mesh axis runs over, the one named last changes fastest.
Arguments:
- emission: bfloat16 [512, 64, 2048], P('depth', 'spec'), may hold values from 0.099609375 to 2
- opacity: bfloat16 [512, 64, 2048], P('depth', 'spec'), may hold values from 0.29882812 to 3
- bin_extinction: float32 [64], P('spec'), may hold values from 0.1 to 30
- entry: int32 [2048], replicated, may hold values from 0 to 127
- exit_cell: int32 [2048], replicated, may hold values from 384 to 512
- response: float32 [3, 64], P(None, 'spec'), may hold values from 0.05 to 1
Outputs:
- nearer_slab_rgb: float32 [16, 3, 2048], P('depth')
- image: float32 [3, 2048], replicated
All inputs are finite; a program needn't handle non-finite values.
Results may differ from a plain program's by a relative error of at most 0.0003.
Values sent between devices are 32-bit elements; how exact they have to be, the bound alone decides.
A program may use at most 64 MiB of HBM per device.

v0:
```python
import jax
import jax.numpy as jnp
from jax import lax
from jax.sharding import PartitionSpec as P


def merge_slabs(earlier, later):
    return (earlier[0] + earlier[1] * later[0], earlier[1] * later[1])


def body(emission, opacity, bin_extinction, entry, exit_cell, response):
    cells = emission.shape[0]
    sections = lax.axis_size("depth")
    cell_step = 1.0 / (cells * sections)
    depth = lax.axis_index("depth") * cells + jnp.arange(cells, dtype=jnp.int32)
    inside = (depth[:, None] >= entry[None, :]) & (depth[:, None] < exit_cell[None, :])
    live = jnp.where(inside, 1.0, 0.0).astype(jnp.float32)
    tau = bin_extinction[None, :, None] * opacity.astype(jnp.float32) * live[:, None, :] * cell_step
    rows = jnp.arange(cells, dtype=jnp.int32)
    lower = jnp.where(rows[None, :] < rows[:, None], 1.0, 0.0).astype(jnp.float32)
    before = jnp.einsum("ij,jbr->ibr", lower, tau, precision=lax.Precision.HIGHEST)
    light = jnp.sum(
        emission.astype(jnp.float32) * live[:, None, :] * cell_step * jnp.exp(-before), axis=0
    )
    trans = jnp.exp(-jnp.sum(tau, axis=0))
    pieces = (
        lax.all_to_all(light[None], "depth", split_axis=2, concat_axis=0, tiled=True),
        lax.all_to_all(trans[None], "depth", split_axis=2, concat_axis=0, tiled=True),
    )
    totals = lax.associative_scan(merge_slabs, (pieces[0], pieces[1]), axis=0)
    lead_light = jnp.concatenate([jnp.zeros_like(pieces[0][:1]), totals[0][:-1]], axis=0)
    lead_trans = jnp.concatenate([jnp.ones_like(pieces[1][:1]), totals[1][:-1]], axis=0)
    moved_light = lax.all_to_all(lead_light, "depth", split_axis=0, concat_axis=2, tiled=True)
    moved_trans = lax.all_to_all(lead_trans, "depth", split_axis=0, concat_axis=2, tiled=True)
    nearer_radiance = moved_light[0]
    nearer_transparency = moved_trans[0]
    front_part = jnp.dot(response, nearer_radiance, precision=lax.Precision.HIGHEST)
    slab_portion = jnp.dot(response, nearer_transparency * light, precision=lax.Precision.HIGHEST)
    nearer_slab_rgb, slab_colour_rgb = lax.psum((front_part, slab_portion), "spec")
    image = lax.psum(slab_colour_rgb, "depth")
    return (nearer_slab_rgb[None], image)


def solution(mesh):
    placed = (
        P("depth", "spec", None),
        P("depth", "spec", None),
        P("spec"),
        P(),
        P(),
        P(None, "spec"),
    )
    return jax.shard_map(
        body, mesh=mesh, in_specs=placed, out_specs=(P("depth", None, None), P()), check_vma=False
    )
```

profile of v0, /device:TPU:0, one launch (start us, length us, event | category | flops | bytes accessed | tf_op | source)
XLA Modules:
  0.0 190.8 jit_solution(17573433646198136472)
XLA Ops:
  0.7 0.8 and_select_fusion
  1.5 5.9 %fusion = f32[32,2048]{1,0:T(8,128)S(1)} fusion(f32[32]{0:T(128)} %param.8, f32[32,2048]{1,0:T(8,128)S(1)} %and_select_fusion, bf16[32,32,2048]{2,1,0:T(8,128)(2,1)} %param.7), kind=kLoop, calls=%fused_computation.2 | loop fusion | flops 10420224 | bytes 4718720 | tf_op jit(solution)/shard_map/reduce_sum | solution.py:25
  7.4 0.6 copy.48
  8.0 0.5 broadcast.88
  8.5 9.3 %reduce = f32[2048,32]{1,0:T(8,128)S(1)} reduce(f32[2048,1,32]{2,1,0:T(1,128)S(1)} %bitcast.63, f32[]{:T(128)} %broadcast.88), dimensions={1}, to_apply=%bitcast.47.reduce_sub_computation | reduce | bytes 524292
  17.9 1.1 reshape.76
  19.0 8.3 %all-to-all-start.1 = ((f32[16,1,4096]{2,1,0:T(1,128)}), f32[16,1,4096]{2,1,0:T(1,128)S(1)}, u32[]{:S(2)}, u32[]{:S(2)}) async-start(f32[16,1,4096]{2,1,0:T(1,128)} %reshape.76), calls=%async_computation.1 | async-start | bytes 524288 | tf_op jit(solution)/shard_map/all_to_all | solution.py:28
  27.4 21.2 %multiply_reduce_fusion = f32[32,2048]{1,0:T(8,128)S(1)} fusion(bf16[32,32,2048]{2,1,0:T(8,128)(2,1)} %param.6, f32[32]{0:T(128)S(1)} %copy-done.1, f32[32,2048]{1,0:T(8,128)S(1)} %and_select_fusion, bf16[32,32,2048]{2,1,0:T(8,128)(2,1)} %param.7), kind=kOutput, calls=%fused_computation | convolution fusion | flops 826214400 | bytes 8913024 | tf_op jit(solution)/shard_map/ij,jbr->ibr/dot_general | solution.py:21
  48.6 0.6 copy.46
  49.2 9.6 %reduce.2 = f32[2048,32]{1,0:T(8,128)S(1)} reduce(f32[2048,1,32]{2,1,0:T(1,128)S(1)} %bitcast.66, f32[]{:T(128)} %broadcast.88), dimensions={1}, to_apply=%bitcast.45.reduce_sub_computation | reduce | bytes 524292
  58.8 1.2 reshape.74
  59.9 6.9 %all-to-all-start = ((f32[16,1,4096]{2,1,0:T(1,128)}), f32[16,1,4096]{2,1,0:T(1,128)S(1)}, u32[]{:S(2)}, u32[]{:S(2)}) async-start(f32[16,1,4096]{2,1,0:T(1,128)} %reshape.74), calls=%async_computation | async-start | bytes 524288 | tf_op jit(solution)/shard_map/all_to_all | solution.py:27
  66.8 1.3 reduce.1
  68.1 1.8 reshape.77
  69.9 0.6 copy.49
  70.9 5.3 %all-to-all-done = f32[16,1,4096]{2,1,0:T(1,128)S(1)} async-done(((f32[16,1,4096]{2,1,0:T(1,128)}), f32[16,1,4096]{2,1,0:T(1,128)S(1)}, u32[]{:S(2)}, u32[]{:S(2)}) %all-to-all-start) | async-done | bytes 262176 | tf_op jit(solution)/shard_map/all_to_all | solution.py:27
  76.2 1.3 reduce.3
  77.4 1.8 reshape.75
  79.3 0.3 copy.57
  81.5 0.4 pad.59
  81.9 0.4 pad.58
  82.4 0.4 pad.56
  82.8 0.4 pad.57
  85.2 0.7 concatenate.31.clone
  85.9 3.5 %all-to-all-start.3 = ((f32[16,32,128]{2,1,0:T(8,128)}), f32[16,32,128]{2,1,0:T(8,128)S(1)}, u32[]{:S(2)}, u32[]{:S(2)}) async-start(f32[16,32,128]{2,1,0:T(8,128)} %concatenate.31.clone), calls=%async_computation.3 | async-start | bytes 524288 | tf_op jit(solution)/shard_map/all_to_all | solution.py:34
  90.1 0.7 concatenate.29.clone
  90.8 7.8 %all-to-all-done.3 = f32[16,32,128]{2,1,0:T(8,128)S(1)} async-done(((f32[16,32,128]{2,1,0:T(8,128)}), f32[16,32,128]{2,1,0:T(8,128)S(1)}, u32[]{:S(2)}, u32[]{:S(2)}) %all-to-all-start.3) | async-done | bytes 262176 | tf_op jit(solution)/shard_map/all_to_all | solution.py:34
  98.7 3.5 %all-to-all-start.2 = ((f32[16,32,128]{2,1,0:T(8,128)}), f32[16,32,128]{2,1,0:T(8,128)S(1)}, u32[]{:S(2)}, u32[]{:S(2)}) async-start(f32[16,32,128]{2,1,0:T(8,128)} %concatenate.29.clone), calls=%async_computation.2 | async-start | bytes 524288 | tf_op jit(solution)/shard_map/all_to_all | solution.py:33
  102.4 9.0 %all-to-all-done.2 = f32[16,32,128]{2,1,0:T(8,128)S(1)} async-done(((f32[16,32,128]{2,1,0:T(8,128)}), f32[16,32,128]{2,1,0:T(8,128)S(1)}, u32[]{:S(2)}, u32[]{:S(2)}) %all-to-all-start.2) | async-done | bytes 262176 | tf_op jit(solution)/shard_map/all_to_all | solution.py:33
  112.2 3.6 %all-reduce.18 = (f32[1,3,2048]{2,1,0:T(4,128)S(1)}, f32[3,2048]{1,0:T(4,128)S(1)}) all-reduce(f32[1,3,2048]{2,1,0:T(4,128)S(1)} %convolution_bitcast_fusion.1, f32[3,2048]{1,0:T(4,128)S(1)} %convolution_bitcast_fusion), channel_id=1, replica_groups=mesh['depth'=16,'spec'=2] {'spec'}, use_global_device_ids=true, to_apply=%region_2.3 | all-reduce | flops 12288 | bytes 98304 | tf_op jit(solution)/shard_map/psum | solution.py:39
  115.8 0.6 copy.56
  116.5 74.4 %psum.23 = f32[3,2048]{1,0:T(4,128)} all-reduce(f32[3,2048]{1,0:T(4,128)S(1)} %get-tuple-element.13), channel_id=1, replica_groups=mesh['depth'=16,'spec'=2] {'depth'}, use_global_device_ids=true, to_apply=%region_4.5 | all-reduce | flops 6144 | bytes 49152 | tf_op jit(solution)/shard_map/psum | solution.py:40
  (61 shorter events, 5.5 us)
Async XLA Ops:
  0.6 110.9 %copy-start = (f32[3,32]{1,0:T(4,128)S(1)}, f32[3,32]{1,0:T(4,128)}, u32[]{:S(2)}) copy-start(f32[3,32]{1,0:T(4,128)} %param.11) | copy-start | bytes 1156
  1.5 25.9 %copy-start.1 = (f32[32]{0:T(128)S(1)}, f32[32]{0:T(128)}, u32[]{:S(2)}) copy-start(f32[32]{0:T(128)} %param.8) | copy-start | bytes 388
  19.0 40.9 %all-to-all-start.1 = ((f32[16,1,4096]{2,1,0:T(1,128)}), f32[16,1,4096]{2,1,0:T(1,128)S(1)}, u32[]{:S(2)}, u32[]{:S(2)}) async-start(f32[16,1,4096]{2,1,0:T(1,128)} %reshape.76), calls=%async_computation.1 | async-start | bytes 524288 | tf_op jit(solution)/shard_map/all_to_all | solution.py:28
  59.9 16.2 %all-to-all-start = ((f32[16,1,4096]{2,1,0:T(1,128)}), f32[16,1,4096]{2,1,0:T(1,128)S(1)}, u32[]{:S(2)}, u32[]{:S(2)}) async-start(f32[16,1,4096]{2,1,0:T(1,128)} %reshape.74), calls=%async_computation | async-start | bytes 524288 | tf_op jit(solution)/shard_map/all_to_all | solution.py:27
  85.9 12.8 %all-to-all-start.3 = ((f32[16,32,128]{2,1,0:T(8,128)}), f32[16,32,128]{2,1,0:T(8,128)S(1)}, u32[]{:S(2)}, u32[]{:S(2)}) async-start(f32[16,32,128]{2,1,0:T(8,128)} %concatenate.31.clone), calls=%async_computation.3 | async-start | bytes 524288 | tf_op jit(solution)/shard_map/all_to_all | solution.py:34
  98.7 12.7 %all-to-all-start.2 = ((f32[16,32,128]{2,1,0:T(8,128)}), f32[16,32,128]{2,1,0:T(8,128)S(1)}, u32[]{:S(2)}, u32[]{:S(2)}) async-start(f32[16,32,128]{2,1,0:T(8,128)} %concatenate.29.clone), calls=%async_computation.2 | async-start | bytes 524288 | tf_op jit(solution)/shard_map/all_to_all | solution.py:33
where the time goes:
time: 192 us; the launch traced here: 191 us
  blocking collectives  78 us (41%)
  other arithmetic  28.9 us (15%)
  starting transfers between devices  22.3 us (12%)
  waiting for transfers between devices  22.1 us (12%)
  matrix products  21.8 us (11%)
  local copies, waits for them, and re-layouts  16.5 us (9%)
    psum x1, blocking collectives, body(): image = lax.psum(slab_colour_rgb, 'depth')  74.4 us
    dot_general x1, matrix products, body(): jnp.einsum('ij,jbr->ibr', lower, tau, precision=lax.Precision.HIGHEST)  21.2 us
    unnamed x2, other arithmetic  18.9 us
    all_to_all x1, waiting for transfers between devices, body(): lax.all_to_all(lead_light, 'depth', split_axis=0, concat_axis=2, tiled=True)  8.99 us
    all_to_all x1, starting transfers between devices, body(): lax.all_to_all(trans[None], 'depth', split_axis=2, concat_axis=0, tiled=T...  8.35 us
    all_to_all x1, waiting for transfers between devices, body(): lax.all_to_all(lead_trans, 'depth', split_axis=0, concat_axis=2, tiled=True)  7.84 us
    unnamed x14, local copies, waits for them, and re-layouts  7.74 us
    all_to_all x1, starting transfers between devices, body(): lax.all_to_all(light[None], 'depth', split_axis=2, concat_axis=0, tiled=T...  6.9 us
  transfers between devices with their start and end apart: 4, of which 3 were waited for; matrix products, arithmetic and copies ran while one was open for 20% of the time, Pallas kernels for 0%

commit v1 on v0

--- a/solution.py
+++ b/solution.py
@@ -37,7 +37,9 @@
     front_part = jnp.dot(response, nearer_radiance, precision=lax.Precision.HIGHEST)
     slab_portion = jnp.dot(response, nearer_transparency * light, precision=lax.Precision.HIGHEST)
     nearer_slab_rgb, slab_colour_rgb = lax.psum((front_part, slab_portion), "spec")
-    image = lax.psum(slab_colour_rgb, "depth")
+    image = slab_colour_rgb
+    for hop in (1, 2, 4, 8):
+        image = image + lax.ppermute(image, "depth", [(dev, dev ^ hop) for dev in range(16)])
     return (nearer_slab_rgb[None], image)
 
 

time: 192 us -> 134 us (0.70)
  blocking collectives: 78 us -> 3.6 us
  waiting for transfers between devices: 22.1 us -> 34.5 us
  starting transfers between devices: 22.3 us -> 26.1 us
    psum x1 -> x0, blocking collectives: 74.4 us -> none  [body(): image = lax.psum(slab_colour_rgb, 'depth')]
    ppermute x0 -> x4, waiting for transfers between devices: none -> 12.4 us  [body(): lax.ppermute(image, 'depth', [(dev, dev ^ hop) for dev in range(16)])]
    ppermute x0 -> x4, starting transfers between devices: none -> 3.77 us  [body(): lax.ppermute(image, 'depth', [(dev, dev ^ hop) for dev in range(16)])]
  transfers between devices with their start and end apart: 4 -> 8, of which waited for: 3 -> 7; matrix products, arithmetic and copies ran while one was open for 20% -> 29% of each run, Pallas kernels for 0% -> 0%
where the time goes in v1:
time: 134 us; the launch traced here: 133 us
  waiting for transfers between devices  34.5 us (26%)
  other arithmetic  29.6 us (22%)
  starting transfers between devices  26.1 us (19%)
  matrix products  21.8 us (16%)
  local copies, waits for them, and re-layouts  16.5 us (12%)
  blocking collectives  3.6 us (3%)
    dot_general x1, matrix products, body(): jnp.einsum('ij,jbr->ibr', lower, tau, precision=lax.Precision.HIGHEST)  21.2 us
    unnamed x2, other arithmetic  18.9 us
    ppermute x4, waiting for transfers between devices, body(): lax.ppermute(image, 'depth', [(dev, dev ^ hop) for dev in range(16)])  12.4 us
    all_to_all x1, waiting for transfers between devices, body(): lax.all_to_all(lead_light, 'depth', split_axis=0, concat_axis=2, tiled=True)  8.98 us
    all_to_all x1, starting transfers between devices, body(): lax.all_to_all(trans[None], 'depth', split_axis=2, concat_axis=0, tiled=T...  8.35 us
    all_to_all x1, waiting for transfers between devices, body(): lax.all_to_all(lead_trans, 'depth', split_axis=0, concat_axis=2, tiled=True)  7.84 us
    unnamed x14, local copies, waits for them, and re-layouts  7.74 us
    all_to_all x1, starting transfers between devices, body(): lax.all_to_all(light[None], 'depth', split_axis=2, concat_axis=0, tiled=T...  6.88 us
  transfers between devices with their start and end apart: 8, of which 7 were waited for; matrix products, arithmetic and copies ran while one was open for 29% of the time, Pallas kernels for 0%

profile of v1, /device:TPU:0, one launch (start us, length us, event | category | flops | bytes accessed | tf_op | source)
XLA Modules:
  0.0 133.3 jit_solution(9755418094442120630)
XLA Ops:
  0.7 0.8 and_select_fusion
  1.5 5.9 %fusion = f32[32,2048]{1,0:T(8,128)S(1)} fusion(f32[32]{0:T(128)} %param.8, f32[32,2048]{1,0:T(8,128)S(1)} %and_select_fusion, bf16[32,32,2048]{2,1,0:T(8,128)(2,1)} %param.7), kind=kLoop, calls=%fused_computation.2 | loop fusion | flops 10420224 | bytes 4718720 | tf_op jit(solution)/shard_map/reduce_sum | solution.py:25
  8.5 9.3 %reduce = f32[2048,32]{1,0:T(8,128)S(1)} reduce(f32[2048,1,32]{2,1,0:T(1,128)S(1)} %bitcast.63, f32[]{:T(128)} %broadcast.88), dimensions={1}, to_apply=%bitcast.47.reduce_sub_computation | reduce | bytes 524292
  17.9 1.1 reshape.76
  19.0 8.3 %all-to-all-start.1 = ((f32[16,1,4096]{2,1,0:T(1,128)}), f32[16,1,4096]{2,1,0:T(1,128)S(1)}, u32[]{:S(2)}, u32[]{:S(2)}) async-start(f32[16,1,4096]{2,1,0:T(1,128)} %reshape.76), calls=%async_computation.1 | async-start | bytes 524288 | tf_op jit(solution)/shard_map/all_to_all | solution.py:28
  27.4 21.2 %multiply_reduce_fusion = f32[32,2048]{1,0:T(8,128)S(1)} fusion(bf16[32,32,2048]{2,1,0:T(8,128)(2,1)} %param.6, f32[32]{0:T(128)S(1)} %copy-done.1, f32[32,2048]{1,0:T(8,128)S(1)} %and_select_fusion, bf16[32,32,2048]{2,1,0:T(8,128)(2,1)} %param.7), kind=kOutput, calls=%fused_computation | convolution fusion | flops 826214400 | bytes 8913024 | tf_op jit(solution)/shard_map/ij,jbr->ibr/dot_general | solution.py:21
  49.2 9.6 %reduce.2 = f32[2048,32]{1,0:T(8,128)S(1)} reduce(f32[2048,1,32]{2,1,0:T(1,128)S(1)} %bitcast.66, f32[]{:T(128)} %broadcast.88), dimensions={1}, to_apply=%bitcast.45.reduce_sub_computation | reduce | bytes 524292
  58.8 1.2 reshape.74
  59.9 6.9 %all-to-all-start = ((f32[16,1,4096]{2,1,0:T(1,128)}), f32[16,1,4096]{2,1,0:T(1,128)S(1)}, u32[]{:S(2)}, u32[]{:S(2)}) async-start(f32[16,1,4096]{2,1,0:T(1,128)} %reshape.74), calls=%async_computation | async-start | bytes 524288 | tf_op jit(solution)/shard_map/all_to_all | solution.py:27
  66.8 1.3 reduce.1
  68.1 1.8 %reshape.77 = f32[2048,1,32]{2,1,0:T(1,128)S(1)} reshape(f32[16,4096]{1,0:T(8,128)S(1)} %reduce.1) | data formatting | bytes 524288
  69.9 0.6 copy.49
  70.9 5.3 %all-to-all-done = f32[16,1,4096]{2,1,0:T(1,128)S(1)} async-done(((f32[16,1,4096]{2,1,0:T(1,128)}), f32[16,1,4096]{2,1,0:T(1,128)S(1)}, u32[]{:S(2)}, u32[]{:S(2)}) %all-to-all-start) | async-done | bytes 262176 | tf_op jit(solution)/shard_map/all_to_all | solution.py:27
  76.1 1.3 reduce.3
  77.4 1.8 %reshape.75 = f32[2048,1,32]{2,1,0:T(1,128)S(1)} reshape(f32[16,4096]{1,0:T(8,128)S(1)} %reduce.3) | data formatting | bytes 524288
  85.1 0.7 concatenate.31.clone
  85.9 3.5 %all-to-all-start.3 = ((f32[16,32,128]{2,1,0:T(8,128)}), f32[16,32,128]{2,1,0:T(8,128)S(1)}, u32[]{:S(2)}, u32[]{:S(2)}) async-start(f32[16,32,128]{2,1,0:T(8,128)} %concatenate.31.clone), calls=%async_computation.3 | async-start | bytes 524288 | tf_op jit(solution)/shard_map/all_to_all | solution.py:34
  90.1 0.7 concatenate.29.clone
  90.8 7.8 %all-to-all-done.3 = f32[16,32,128]{2,1,0:T(8,128)S(1)} async-done(((f32[16,32,128]{2,1,0:T(8,128)}), f32[16,32,128]{2,1,0:T(8,128)S(1)}, u32[]{:S(2)}, u32[]{:S(2)}) %all-to-all-start.3) | async-done | bytes 262176 | tf_op jit(solution)/shard_map/all_to_all | solution.py:34
  98.7 3.5 %all-to-all-start.2 = ((f32[16,32,128]{2,1,0:T(8,128)}), f32[16,32,128]{2,1,0:T(8,128)S(1)}, u32[]{:S(2)}, u32[]{:S(2)}) async-start(f32[16,32,128]{2,1,0:T(8,128)} %concatenate.29.clone), calls=%async_computation.2 | async-start | bytes 524288 | tf_op jit(solution)/shard_map/all_to_all | solution.py:33
  102.4 9.0 %all-to-all-done.2 = f32[16,32,128]{2,1,0:T(8,128)S(1)} async-done(((f32[16,32,128]{2,1,0:T(8,128)}), f32[16,32,128]{2,1,0:T(8,128)S(1)}, u32[]{:S(2)}, u32[]{:S(2)}) %all-to-all-start.2) | async-done | bytes 262176 | tf_op jit(solution)/shard_map/all_to_all | solution.py:33
  112.2 3.6 %all-reduce.18 = (f32[1,3,2048]{2,1,0:T(4,128)S(1)}, f32[3,2048]{1,0:T(4,128)S(1)}) all-reduce(f32[1,3,2048]{2,1,0:T(4,128)S(1)} %convolution_bitcast_fusion.1, f32[3,2048]{1,0:T(4,128)S(1)} %convolution_bitcast_fusion), channel_id=1, replica_groups=mesh['depth'=16,'spec'=2] {'spec'}, use_global_device_ids=true, to_apply=%region_2.3 | all-reduce | flops 12288 | bytes 98304 | tf_op jit(solution)/shard_map/psum | solution.py:39
  115.8 0.9 collective-permute-start
  116.6 3.1 %collective-permute-done = f32[3,2048]{1,0:T(4,128)S(1)} collective-permute-done((f32[3,2048]{1,0:T(4,128)S(1)}, f32[3,2048]{1,0:T(4,128)S(1)}, u32[]{:S(2)}, u32[]{:S(2)}) %collective-permute-start) | collective-permute-done | bytes 24608 | tf_op jit(solution)/shard_map/ppermute | solution.py:42
  119.8 1.0 collective-permute-start.1
  120.8 3.0 %collective-permute-done.1 = f32[3,2048]{1,0:T(4,128)S(1)} collective-permute-done((f32[3,2048]{1,0:T(4,128)S(1)}, f32[3,2048]{1,0:T(4,128)S(1)}, u32[]{:S(2)}, u32[]{:S(2)}) %collective-permute-start.1) | collective-permute-done | bytes 24608 | tf_op jit(solution)/shard_map/ppermute | solution.py:42
  123.8 1.2 collective-permute-start.2
  124.9 2.8 %collective-permute-done.2 = f32[3,2048]{1,0:T(4,128)S(1)} collective-permute-done((f32[3,2048]{1,0:T(4,128)S(1)}, f32[3,2048]{1,0:T(4,128)S(1)}, u32[]{:S(2)}, u32[]{:S(2)}) %collective-permute-start.2) | collective-permute-done | bytes 24608 | tf_op jit(solution)/shard_map/ppermute | solution.py:42
  127.8 0.8 collective-permute-start.3
  128.6 0.6 copy.56
  129.2 3.5 %collective-permute-done.3 = f32[3,2048]{1,0:T(4,128)S(1)} collective-permute-done((f32[3,2048]{1,0:T(4,128)S(1)}, f32[3,2048]{1,0:T(4,128)S(1)}, u32[]{:S(2)}, u32[]{:S(2)}) %collective-permute-start.3) | collective-permute-done | bytes 24608 | tf_op jit(solution)/shard_map/ppermute | solution.py:42
  132.7 0.6 add.127
  (72 shorter events, 9.3 us)
Async XLA Ops:
  0.6 110.9 %copy-start = (f32[3,32]{1,0:T(4,128)S(1)}, f32[3,32]{1,0:T(4,128)}, u32[]{:S(2)}) copy-start(f32[3,32]{1,0:T(4,128)} %param.11) | copy-start | bytes 1156
  1.5 25.9 %copy-start.1 = (f32[32]{0:T(128)S(1)}, f32[32]{0:T(128)}, u32[]{:S(2)}) copy-start(f32[32]{0:T(128)} %param.8) | copy-start | bytes 388
  19.0 40.9 %all-to-all-start.1 = ((f32[16,1,4096]{2,1,0:T(1,128)}), f32[16,1,4096]{2,1,0:T(1,128)S(1)}, u32[]{:S(2)}, u32[]{:S(2)}) async-start(f32[16,1,4096]{2,1,0:T(1,128)} %reshape.76), calls=%async_computation.1 | async-start | bytes 524288 | tf_op jit(solution)/shard_map/all_to_all | solution.py:28
  59.9 16.2 %all-to-all-start = ((f32[16,1,4096]{2,1,0:T(1,128)}), f32[16,1,4096]{2,1,0:T(1,128)S(1)}, u32[]{:S(2)}, u32[]{:S(2)}) async-start(f32[16,1,4096]{2,1,0:T(1,128)} %reshape.74), calls=%async_computation | async-start | bytes 524288 | tf_op jit(solution)/shard_map/all_to_all | solution.py:27
  85.9 12.8 %all-to-all-start.3 = ((f32[16,32,128]{2,1,0:T(8,128)}), f32[16,32,128]{2,1,0:T(8,128)S(1)}, u32[]{:S(2)}, u32[]{:S(2)}) async-start(f32[16,32,128]{2,1,0:T(8,128)} %concatenate.31.clone), calls=%async_computation.3 | async-start | bytes 524288 | tf_op jit(solution)/shard_map/all_to_all | solution.py:34
  98.7 12.7 %all-to-all-start.2 = ((f32[16,32,128]{2,1,0:T(8,128)}), f32[16,32,128]{2,1,0:T(8,128)S(1)}, u32[]{:S(2)}, u32[]{:S(2)}) async-start(f32[16,32,128]{2,1,0:T(8,128)} %concatenate.29.clone), calls=%async_computation.2 | async-start | bytes 524288 | tf_op jit(solution)/shard_map/all_to_all | solution.py:33
  115.8 4.0 %collective-permute-start = (f32[3,2048]{1,0:T(4,128)S(1)}, f32[3,2048]{1,0:T(4,128)S(1)}, u32[]{:S(2)}, u32[]{:S(2)}) collective-permute-start(f32[3,2048]{1,0:T(4,128)S(1)} %get-tuple-element.13), channel_id=1, source_target_pairs={{0,2},{2,0},{4,6},{6,4},{8,10},{10,8},{12,14},{14,12},{16,18},{18,... | collective-permute-start | bytes 73736 | tf_op jit(solution)/shard_map/ppermute | solution.py:42
  119.8 4.0 %collective-permute-start.1 = (f32[3,2048]{1,0:T(4,128)S(1)}, f32[3,2048]{1,0:T(4,128)S(1)}, u32[]{:S(2)}, u32[]{:S(2)}) collective-permute-start(f32[3,2048]{1,0:T(4,128)S(1)} %add.124), channel_id=1, source_target_pairs={{0,4},{2,6},{4,0},{6,2},{8,12},{10,14},{12,8},{14,10},{16,20},{18,... | collective-permute-start | bytes 73736 | tf_op jit(solution)/shard_map/ppermute | solution.py:42
  123.8 4.0 %collective-permute-start.2 = (f32[3,2048]{1,0:T(4,128)S(1)}, f32[3,2048]{1,0:T(4,128)S(1)}, u32[]{:S(2)}, u32[]{:S(2)}) collective-permute-start(f32[3,2048]{1,0:T(4,128)S(1)} %add.125), channel_id=1, source_target_pairs={{0,8},{2,10},{4,12},{6,14},{8,0},{10,2},{12,4},{14,6},{16,24},{18,... | collective-permute-start | bytes 73736 | tf_op jit(solution)/shard_map/ppermute | solution.py:42
  127.8 4.9 %collective-permute-start.3 = (f32[3,2048]{1,0:T(4,128)S(1)}, f32[3,2048]{1,0:T(4,128)S(1)}, u32[]{:S(2)}, u32[]{:S(2)}) collective-permute-start(f32[3,2048]{1,0:T(4,128)S(1)} %add.126), channel_id=1, source_target_pairs={{0,16},{2,18},{4,20},{6,22},{8,24},{10,26},{12,28},{14,30},{16,0},... | collective-permute-start | bytes 73736 | tf_op jit(solution)/shard_map/ppermute | solution.py:42
